TPU v7x, 256 devices: a whole 4x4x8 slice. The times are simulated.
256 devices in a mesh: store: 16 (over z_lo, y), seq: 16 (over z_hi, x, core).
Axes of the slice: x: 4, y: 4, z: 8 (z_hi: 2, z_lo: 4; z = z_hi * 4 + z_lo), core: 2. Of those that a mesh axis runs over, the one named last changes fastest.
Arguments:
- store_kv: bfloat16 [256, 640, 2048], P('store', 'seq'), may hold values from -8 to 8
- span_len: int32 [16, 144], replicated, may hold values from 18 to 40, as said below
- span_shard: int32 [16, 16], replicated, may hold values from 0 to 15, each once within a row
- q_sel: bfloat16 [16, 1024, 8192], P('store', 'seq'), may hold values from -8 to 8
- fresh_kv: bfloat16 [16, 1024, 2048], P('store', 'seq'), may hold values from -8 to 8
- sel_pos: int32 [16, 1024], P('store', 'seq'), may hold values from -1 to 4095, as said below
Outputs:
- blended_kv: bfloat16 [16, 4096, 2048], P('store', 'seq')
- attn_out: bfloat16 [16, 1024, 8192], P('store', 'seq')
Inputs may be any that keep to these rules, and one draw needn't show every extreme that they name: `span_len`: each row sums to 4096, and its largest entry is 40. `span_shard`: each row names every store shard once. `sel_pos`: on seq index q, the 64 slots of a request hold distinct positions from q * 256 to (q + 1) * 256 - 1 in rising order, then -1 in unused slots; at least 2 slots are used, and in every draw some device uses all 64.
All inputs are finite; a program needn't handle non-finite values.
Results may differ from a plain program's by a relative error of at most 0.007.
Values may be sent and summed in bfloat16 or wider, within the bound.
No kernel may reach another device: no remote copies, remote signals or barrier semaphores. Data moves between devices by JAX's collectives and lax.ppermute only.
A program may use at most 192 MiB of HBM per device.

v0:
```python
import math
import jax
import jax.numpy as jnp
from jax import lax
from jax.sharding import PartitionSpec as P

HEADS = 64
KV_HEADS = 8
D_HEAD = 128
TOK_DEV = 256
ROPE_BASE = 500000.0


def rotate_keys(kv_rows, span_start):
    half_dim = D_HEAD // 2
    kv_width = KV_HEADS * D_HEAD
    row_count = kv_rows.shape[0]
    inverse = jnp.power(ROPE_BASE, -(jnp.arange(half_dim, dtype=jnp.float32) * 2.0 / D_HEAD))
    angles = span_start.astype(jnp.float32)[:, None] * inverse[None, :]
    cosine = jnp.cos(angles)[:, None, :]
    sine_part = jnp.sin(angles)[:, None, :]
    key_rows = kv_rows[:, :kv_width].reshape(row_count, KV_HEADS, D_HEAD)
    lower_half = key_rows[..., :half_dim]
    upper_half = key_rows[..., half_dim:]
    turned = jnp.concatenate(
        [
            lower_half * cosine - upper_half * sine_part,
            upper_half * cosine + lower_half * sine_part,
        ],
        axis=2,
    )
    return jnp.concatenate([turned.reshape(row_count, kv_width), kv_rows[:, kv_width:]], axis=1)


def locate(span_lengths, span_holders, positions):
    span_starts = jnp.cumsum(span_lengths) - span_lengths
    span_ids = jnp.arange(span_lengths.shape[0], dtype=jnp.int32)
    inside = (positions[:, None] >= span_starts[None, :]).astype(jnp.int32)
    which_span = jnp.sum(inside, axis=1) - 1
    picked = (which_span[:, None] == span_ids[None, :]).astype(jnp.int32)
    holder = jnp.sum(picked * span_holders[None, :], axis=1)
    span_start = jnp.sum(picked * span_starts[None, :], axis=1)
    return (holder, span_start)


def empty_states(row_count):
    groups = HEADS // KV_HEADS
    return (
        jnp.full((KV_HEADS, groups, row_count), -1e30, jnp.float32),
        jnp.zeros((KV_HEADS, groups, row_count), jnp.float32),
        jnp.zeros((KV_HEADS, groups, row_count, D_HEAD), jnp.float32),
    )


def absorb(states, queries, limits, kv_piece, first_row):

    def update(current):
        running_max, running_sum, weighted = current
        row_count = kv_piece.shape[0]
        kv_width = KV_HEADS * D_HEAD
        key_rows = kv_piece[:, :kv_width].reshape(row_count, KV_HEADS, D_HEAD)
        value_rows = kv_piece[:, kv_width:].reshape(row_count, KV_HEADS, D_HEAD)
        grouped = queries.reshape(queries.shape[0], KV_HEADS, HEADS // KV_HEADS, D_HEAD)
        scores = jnp.einsum(
            "qhgd,khd->hgqk", grouped, key_rows, preferred_element_type=jnp.float32
        ) / math.sqrt(D_HEAD)
        key_positions = jnp.arange(row_count, dtype=jnp.int32)
        allowed = (key_positions[None, :] <= limits[:, None])[None, None]
        piece_max = jnp.max(jnp.where(allowed, scores, -jnp.inf), axis=3)
        raised = jnp.maximum(running_max, piece_max)
        weights = jnp.where(allowed, jnp.exp(scores - raised[..., None]), 0.0)
        running_sum = jnp.sum(weights, axis=3)
        weighted = jnp.einsum(
            "hgqk,khd->hgqd",
            weights.astype(jnp.bfloat16),
            value_rows,
            preferred_element_type=jnp.float32,
        )
        return (raised, running_sum, weighted)

    useful = (first_row >= 0) & (first_row <= jnp.max(limits))
    return lax.cond(useful, update, lambda current: current, states)


def finish(states):
    running_max, running_sum, weighted = states
    normed = weighted / running_sum[..., None]
    return jnp.transpose(normed, (2, 0, 1, 3)).reshape(normed.shape[2], HEADS * D_HEAD)


def on_device(store_kv, span_len, span_shard, q_sel, fresh_kv, sel_pos):
    slot_rows = store_kv.shape[1]
    request = lax.axis_index("store")
    stripe = lax.axis_index("seq")
    fetched = lax.all_to_all(store_kv, "store", split_axis=0, concat_axis=0, tiled=True)
    lengths_row = lax.dynamic_index_in_dim(span_len, request, 0, keepdims=False)
    shards_row = lax.dynamic_index_in_dim(span_shard, request, 0, keepdims=False)
    holders_row = jnp.tile(shards_row, span_len.shape[1] // span_shard.shape[1])
    positions = stripe * TOK_DEV + jnp.arange(TOK_DEV, dtype=jnp.int32)
    holder, span_start = locate(lengths_row, holders_row, positions)
    offset = positions - jnp.maximum(span_start, stripe * TOK_DEV)
    flat_rows = fetched.reshape(-1, fetched.shape[2])
    cached = jnp.take(flat_rows, holder * slot_rows + offset, axis=0)
    rotated = rotate_keys(cached.astype(jnp.float32), span_start)
    chosen = sel_pos[0]
    matches = positions[:, None] == chosen[None, :]
    fresh_rows = jnp.dot(
        matches.astype(jnp.bfloat16), fresh_kv[0], preferred_element_type=jnp.float32
    )
    blended = jnp.where(jnp.any(matches, axis=1)[:, None], fresh_rows, rotated).astype(jnp.bfloat16)
    queries = q_sel[0]
    limits = jnp.maximum(chosen, 0)
    groups = ((queries, limits),)
    initial = tuple((empty_states(member[0].shape[0]) for member in groups))
    kv_piece = lax.all_gather(blended, "seq", axis=0, tiled=True)
    first_row = jnp.int32(0)
    finished = tuple(
        (
            absorb(member_state, member[0], member[1], kv_piece, first_row)
            for member_state, member in zip(initial, groups)
        )
    )
    attention = finish(finished[0]).astype(jnp.bfloat16)
    attended = jnp.where((chosen >= 0)[:, None], attention, jnp.zeros_like(attention))
    return (blended[None], attended[None])


def solution(mesh):
    return jax.shard_map(
        on_device,
        mesh=mesh,
        in_specs=(
            P("store", "seq", None),
            P(),
            P(),
            P("store", "seq", None),
            P("store", "seq", None),
            P("store", "seq"),
        ),
        out_specs=(P("store", "seq", None), P("store", "seq", None)),
        check_vma=False,
    )
```

profile of v0, /device:TPU:1, one launch (start us, length us, event | category | flops | bytes accessed | tf_op | source)
XLA Modules:
  0.0 371.7 jit_solution(6813124720219924720)
XLA Ops:
  7.2 9.3 %all-to-all-start = ((bf16[16,40,2048]{2,1,0:T(8,128)(2,1)}), bf16[16,40,2048]{2,1,0:T(8,128)(2,1)S(1)}, u32[]{:S(2)}, u32[]{:S(2)}) async-start(bf16[16,40,2048]{2,1,0:T(8,128)(2,1)} %param.8), calls=%async_computation | async-start | bytes 5242880 | tf_op jit(solution)/shard_map/all_to_all | solution.py:95
  16.6 0.7 constant_dynamic-slice_fusion
  17.3 0.3 reduce-window.9
  17.7 0.7 dynamic-slice_bitcast_fusion
  19.0 0.7 compare_reduce_fusion
  19.8 0.5 multiply_cosine_fusion
  20.3 46.9 %all-to-all-done = bf16[16,40,2048]{2,1,0:T(8,128)(2,1)S(1)} async-done(((bf16[16,40,2048]{2,1,0:T(8,128)(2,1)}), bf16[16,40,2048]{2,1,0:T(8,128)(2,1)S(1)}, u32[]{:S(2)}, u32[]{:S(2)}) %all-to-all-start) | async-done | bytes 2621472 | tf_op jit(solution)/shard_map/all_to_all | solution.py:95
  67.2 2.3 gather_fusion
  69.5 1.4 select_convert_fusion
  71.3 0.5 multiply_subtract_fusion
  71.8 0.3 pad_maximum_fusion
  72.3 1.5 fusion.12
  73.8 0.6 broadcast_maximum_fusion.2
  75.1 182.5 %all-gather.2.cloned.1.call-done = bf16[4096,2048]{1,0:T(8,128)(2,1)} async-done(((bf16[256,2048]{1,0:T(8,128)(2,1)}), bf16[4096,2048]{1,0:T(8,128)(2,1)}) %all-gather.2.cloned.1.call-update) | async-done | bytes 16777232 | tf_op jit(solution)/shard_map/all_gather | solution.py:115
  257.6 103.0 %conditional.1 = (f32[8,8,64]{2,1,0:T(8,128)S(1)}, f32[8,8,64,128]{3,2,1,0:T(8,128)}) conditional(s32[]{:T(128)} %convert_element_type.44, () %tuple.16, (s32[64]{0:T(128)S(1)}, bf16[4096,2048]{1,0:T(8,128)(2,1)}, bf16[1,64,8192]{2,1,0:T(8,128)(2,1)}) %tuple.17), branch_computations={%region_7.8_spmd, %region_8.11_spmd} | conditional | flops 8774742016 | bytes 295797056 | solution.py:82
  257.8 20.7 %copy.19 = bf16[4096,2048]{0,1:T(8,128)(2,1)} copy(bf16[4096,2048]{1,0:T(8,128)(2,1)} %get-tuple-element.21) | data formatting | bytes 33554432 | tf_op jit(solution)/shard_map
  278.5 9.5 %fusion.19 = (bf16[4096,1024]{0,1:T(8,128)(2,1)}, bf16[4096,1024]{0,1:T(8,128)(2,1)S(1)}) fusion(bf16[4096,2048]{0,1:T(8,128)(2,1)} %copy.19), kind=kLoop, calls=%fused_computation.56 | loop fusion | bytes 33554432 | tf_op jit(solution)/shard_map/cond/branch_1_fun/slice | solution.py:62
  288.3 23.6 %fusion = (f32[8,8,64]{2,1,0:T(8,128)S(1)}, f32[8,4096,64,8]{1,2,3,0:T(8,128)}) fusion(pred[64,4096]{1,0:T(8,128)(4,1)S(1)} %iota_compare_fusion, bf16[4096,8,128,1]{0,2,3,1:T(8,128)(2,1)S(1)} %bitcast.62, bf16[64,8,8,128]{3,2,1,0:T(8,128)(2,1)S(1)} %bitcast.65), kind=kOutput, calls=%fused_computation.3 | convolution fusion | flops 4345294848 | bytes 76824576 | tf_op jit(solution)/shard_map/cond/branch_1_fun/qhgd,khd->hgqk/dot_general | solution.py:64
  311.9 27.0 %fusion.5 = f32[8,8,64,128]{3,2,1,0:T(8,128)} fusion(bf16[4096,8,128,1]{0,2,3,1:T(8,128)(2,1)} %bitcast.64, f32[8,4096,64,8]{1,2,3,0:T(8,128)} %get-tuple-element.30, f32[8,8,64]{2,1,0:T(8,128)S(1)} %broadcast_maximum_fusion, pred[64,4096]{1,0:T(8,128)(4,1)S(1)} %iota_compare_fusion), kind=kOutput, calls=%fused_computation.8 | convolution fusion | flops 4362076160 | bytes 77873152 | tf_op jit(solution)/shard_map/cond/branch_1_fun/hgqk,khd->hgqd/dot_general | solution.py:73
  338.9 21.6 %fusion.4 = f32[8,8,64]{2,1,0:T(8,128)S(1)} fusion(f32[8,4096,64,8]{1,2,3,0:T(8,128)} %get-tuple-element.30, f32[8,8,64]{2,1,0:T(8,128)S(1)} %broadcast_maximum_fusion, pred[64,4096]{1,0:T(8,128)(4,1)S(1)} %iota_compare_fusion), kind=kLoop, calls=%fused_computation.7 | loop fusion | flops 67104768 | bytes 67403776 | tf_op jit(solution)/shard_map/cond/branch_1_fun/reduce_sum | solution.py:72
  360.6 2.0 fusion.13
  362.6 0.7 copy.20
  363.3 0.5 convert_element_type.47
  363.8 1.1 broadcast_select_fusion
  (36 shorter events, 1.7 us)
Async XLA Ops:
  7.2 65.1 %copy-start = (bf16[1,64,2048]{2,1,0:T(8,128)(2,1)S(1)}, bf16[1,64,2048]{2,1,0:T(8,128)(2,1)}, u32[]{:S(2)}) copy-start(bf16[1,64,2048]{2,1,0:T(8,128)(2,1)} %param.12) | copy-start | bytes 786436
  7.2 65.1 %copy-start.3 = (s32[1,64]{1,0:T(1,128)S(1)}, s32[1,64]{1,0:T(1,128)}, u32[]{:S(2)}) copy-start(s32[1,64]{1,0:T(1,128)} %param.13) | copy-start | bytes 772
  7.2 60.0 %all-to-all-start = ((bf16[16,40,2048]{2,1,0:T(8,128)(2,1)}), bf16[16,40,2048]{2,1,0:T(8,128)(2,1)S(1)}, u32[]{:S(2)}, u32[]{:S(2)}) async-start(bf16[16,40,2048]{2,1,0:T(8,128)(2,1)} %param.8), calls=%async_computation | async-start | bytes 5242880 | tf_op jit(solution)/shard_map/all_to_all | solution.py:95
  16.5 241.0 %all-gather.2.cloned.1.call-start = ((), (), s32[]{:S(2)}) async-start(), calls=%async_computation.1 | async-start | bytes 17825792 | tf_op jit(solution)/shard_map/all_gather | solution.py:115
  278.5 9.5 %copy-start.2 = (bf16[1,64,8192]{2,1,0:T(8,128)(2,1)S(1)}, bf16[1,64,8192]{2,1,0:T(8,128)(2,1)}, u32[]{:S(2)}) copy-start(bf16[1,64,8192]{2,1,0:T(8,128)(2,1)} %get-tuple-element.16) | copy-start | bytes 3145732 | tf_op jit(solution)/shard_map/cond
  360.6 4.3 %copy-start.1 = (bf16[1,64,2048]{2,1,0:T(8,128)(2,1)S(1)}, bf16[1,64,2048]{2,1,0:T(8,128)(2,1)}, u32[]{:S(2)}) copy-start(bf16[1,64,2048]{2,1,0:T(8,128)(2,1)} %param.12) | copy-start | bytes 786436
Sparse Core Ops, SparseCore 0:
  73.9 183.5 all-gather.1
where the time goes:
time: 373 us; the launch traced here: 372 us
  waiting for transfers between devices  229 us (61%)
  matrix products  52.2 us (14%)
  local copies, waits for them, and re-layouts  36.2 us (10%)
  other arithmetic  29.8 us (8%)
  between operations  14.9 us (4%)
  starting transfers between devices  9.36 us (3%)
    all_gather x1, waiting for transfers between devices, on_device(): kv_piece = lax.all_gather(blended, 'seq', axis=0, tiled=True)  182 us
    all_to_all x1, waiting for transfers between devices, on_device(): lax.all_to_all(store_kv, 'store', split_axis=0, concat_axis=0, tiled=True)  46.9 us
    dot_general x1, matrix products, update(): jnp.einsum('hgqk,khd->hgqd', weights.astype(jnp.bfloat16), value_rows, pr...  27 us
    dot_general x1, matrix products, update(): jnp.einsum('qhgd,khd->hgqk', grouped, key_rows, preferred_element_type=jn...  23.6 us
    reduce_sum x1, other arithmetic, update(): running_sum = jnp.sum(weights, axis=3)  21.6 us
    another operation x2, local copies, waits for them, and re-layouts  20.9 us
    slice x1, local copies, waits for them, and re-layouts, update(): value_rows = kv_piece[:, kv_width:].reshape(row_count, KV_HEADS, D_HEAD)  9.49 us
    all_to_all x1, starting transfers between devices, on_device(): lax.all_to_all(store_kv, 'store', split_axis=0, concat_axis=0, tiled=True)  9.32 us
  transfers between devices with their start and end apart: 2, of which 2 were waited for; matrix products, arithmetic and copies ran while one was open for 1% of the time, Pallas kernels for 0%

commit v1 on v0

--- a/solution.py
+++ b/solution.py
@@ -112,7 +112,13 @@
     limits = jnp.maximum(chosen, 0)
     groups = ((queries, limits),)
     initial = tuple((empty_states(member[0].shape[0]) for member in groups))
-    kv_piece = lax.all_gather(blended, "seq", axis=0, tiled=True)
+    plan_the_groups = lambda piece_in: jnp.concatenate(
+        lax.all_to_all(
+            jnp.stack([piece_in for _ in range(lax.psum(1, "seq"))], axis=0), "seq", 0, 0
+        ),
+        axis=0,
+    )
+    kv_piece = plan_the_groups(blended)
     first_row = jnp.int32(0)
     finished = tuple(
         (

time: 373 us -> 665 us (1.78)
  the two profiles are of different devices: /device:TPU:1 before, /device:TPU:87 now
where the time goes in v1:
time: 665 us; the launch traced here: 664 us
  waiting for transfers between devices  539 us (81%)
  matrix products  51.2 us (8%)
  other arithmetic  29.8 us (4%)
  local copies, waits for them, and re-layouts  25.3 us (4%)
  starting transfers between devices  17.3 us (3%)
    all_to_all x1, waiting for transfers between devices, on_device(): lax.all_to_all(jnp.stack([piece_in for _ in range(lax.psum(1, 'seq'))], a...  486 us
    all_to_all x1, waiting for transfers between devices, on_device(): lax.all_to_all(store_kv, 'store', split_axis=0, concat_axis=0, tiled=True)  52.8 us
    dot_general x1, matrix products, update(): jnp.einsum('hgqk,khd->hgqd', weights.astype(jnp.bfloat16), value_rows, pr...  27 us
    dot_general x1, matrix products, update(): jnp.einsum('qhgd,khd->hgqk', grouped, key_rows, preferred_element_type=jn...  23.6 us
    reduce_sum x1, other arithmetic, update(): running_sum = jnp.sum(weights, axis=3)  21.6 us
  transfers between devices with their start and end apart: 2, of which 2 were waited for; matrix products, arithmetic and copies ran while one was open for 1% of the time, Pallas kernels for 0%

profile of v1, /device:TPU:87, one launch (start us, length us, event | category | flops | bytes accessed | tf_op | source)
XLA Modules:
  0.0 664.4 jit_solution(1468505054324442799)
XLA Ops:
  0.7 7.6 %all-to-all-start = ((bf16[16,40,2048]{2,1,0:T(8,128)(2,1)}), bf16[16,40,2048]{2,1,0:T(8,128)(2,1)S(1)}, u32[]{:S(2)}, u32[]{:S(2)}) async-start(bf16[16,40,2048]{2,1,0:T(8,128)(2,1)} %param.8), calls=%async_computation | async-start | bytes 5242880 | tf_op jit(solution)/shard_map/all_to_all | solution.py:95
  8.2 0.7 constant_dynamic-slice_fusion
  9.3 0.7 dynamic-slice_bitcast_fusion
  10.6 0.7 compare_reduce_fusion
  11.4 0.5 multiply_cosine_fusion
  11.9 52.8 %all-to-all-done = bf16[16,40,2048]{2,1,0:T(8,128)(2,1)S(1)} async-done(((bf16[16,40,2048]{2,1,0:T(8,128)(2,1)}), bf16[16,40,2048]{2,1,0:T(8,128)(2,1)S(1)}, u32[]{:S(2)}, u32[]{:S(2)}) %all-to-all-start) | async-done | bytes 2621472 | tf_op jit(solution)/shard_map/all_to_all | solution.py:95
  64.8 2.3 gather_fusion
  67.1 1.4 select_convert_fusion
  68.9 0.5 multiply_subtract_fusion
  69.9 0.5 fusion.12
  70.4 0.5 copy.25
  70.9 6.1 stack.2
  77.0 9.7 %all-to-all-start.1 = ((bf16[16,256,2048]{1,2,0:T(8,128)(2,1)}), bf16[16,256,2048]{1,2,0:T(8,128)(2,1)}, u32[]{:S(2)}, u32[]{:S(2)}) async-start(bf16[16,256,2048]{1,2,0:T(8,128)(2,1)} %stack.2), calls=%async_computation.1 | async-start | bytes 33554432 | tf_op jit(solution)/shard_map/all_to_all | solution.py:116
  86.8 0.6 broadcast_maximum_fusion.2
  88.1 486.4 %all-to-all-done.1 = bf16[16,256,2048]{1,2,0:T(8,128)(2,1)} async-done(((bf16[16,256,2048]{1,2,0:T(8,128)(2,1)}), bf16[16,256,2048]{1,2,0:T(8,128)(2,1)}, u32[]{:S(2)}, u32[]{:S(2)}) %all-to-all-start.1) | async-done | bytes 16777248 | tf_op jit(solution)/shard_map/all_to_all | solution.py:116
  574.5 85.6 %conditional.1 = (f32[8,8,64]{2,1,0:T(8,128)S(1)}, f32[8,8,64,128]{3,2,1,0:T(8,128)}) conditional(s32[]{:T(128)} %convert_element_type.44, () %tuple.16, (s32[64]{0:T(128)S(1)}, bf16[16,256,2048]{1,2,0:T(8,128)(2,1)}, bf16[1,64,8192]{2,1,0:T(8,128)(2,1)}) %tuple.17), branch_computations={%region_7.8_spmd, %region_8.11_spmd} | conditional | flops 8774742016 | bytes 295797056 | solution.py:82
  574.7 8.5 %copy.34 = bf16[16,256,8,256]{3,2,0,1:T(8,128)(2,1)S(1)} copy(bf16[16,256,8,256]{3,2,1,0:T(8,128)(2,1)} %bitcast.23) | data formatting | bytes 33554432 | tf_op jit(solution)/shard_map/reshape | solution.py:115
  583.2 4.3 fusion.19
  587.8 23.6 %fusion = (f32[8,8,64]{2,1,0:T(8,128)S(1)}, f32[8,4096,64,8]{1,2,3,0:T(8,128)}) fusion(pred[64,4096]{1,0:T(8,128)(4,1)S(1)} %iota_compare_fusion, bf16[4096,8,128,1]{0,2,3,1:T(8,128)(2,1)S(1)} %bitcast.65, bf16[64,8,8,128]{3,2,1,0:T(8,128)(2,1)S(1)} %bitcast.68), kind=kOutput, calls=%fused_computation.3 | convolution fusion | flops 4345294848 | bytes 76824576 | tf_op jit(solution)/shard_map/cond/branch_1_fun/qhgd,khd->hgqk/dot_general | solution.py:64
  611.4 27.0 %fusion.5 = f32[8,8,64,128]{3,2,1,0:T(8,128)} fusion(bf16[4096,8,128,1]{0,2,3,1:T(8,128)(2,1)} %bitcast.67, f32[8,4096,64,8]{1,2,3,0:T(8,128)} %get-tuple-element.31, f32[8,8,64]{2,1,0:T(8,128)S(1)} %broadcast_maximum_fusion, pred[64,4096]{1,0:T(8,128)(4,1)S(1)} %iota_compare_fusion), kind=kOutput, calls=%fused_computation.8 | convolution fusion | flops 4362076160 | bytes 77873152 | tf_op jit(solution)/shard_map/cond/branch_1_fun/hgqk,khd->hgqd/dot_general | solution.py:73
  638.4 21.6 %fusion.4 = f32[8,8,64]{2,1,0:T(8,128)S(1)} fusion(f32[8,4096,64,8]{1,2,3,0:T(8,128)} %get-tuple-element.31, f32[8,8,64]{2,1,0:T(8,128)S(1)} %broadcast_maximum_fusion, pred[64,4096]{1,0:T(8,128)(4,1)S(1)} %iota_compare_fusion), kind=kLoop, calls=%fused_computation.7 | loop fusion | flops 67104768 | bytes 67403776 | tf_op jit(solution)/shard_map/cond/branch_1_fun/reduce_sum | solution.py:72
  660.1 2.0 fusion.13
  662.1 0.7 copy.27
  663.3 1.1 broadcast_select_fusion
  (39 shorter events, 2.8 us)
Async XLA Ops:
  0.6 69.2 %copy-start = (bf16[1,64,2048]{2,1,0:T(8,128)(2,1)S(1)}, bf16[1,64,2048]{2,1,0:T(8,128)(2,1)}, u32[]{:S(2)}) copy-start(bf16[1,64,2048]{2,1,0:T(8,128)(2,1)} %param.12) | copy-start | bytes 786436
  0.6 69.2 %copy-start.4 = (s32[1,64]{1,0:T(1,128)S(1)}, s32[1,64]{1,0:T(1,128)}, u32[]{:S(2)}) copy-start(s32[1,64]{1,0:T(1,128)} %param.13) | copy-start | bytes 772
  0.7 64.1 %all-to-all-start = ((bf16[16,40,2048]{2,1,0:T(8,128)(2,1)}), bf16[16,40,2048]{2,1,0:T(8,128)(2,1)S(1)}, u32[]{:S(2)}, u32[]{:S(2)}) async-start(bf16[16,40,2048]{2,1,0:T(8,128)(2,1)} %param.8), calls=%async_computation | async-start | bytes 5242880 | tf_op jit(solution)/shard_map/all_to_all | solution.py:95
  70.4 6.6 copy-start.3
  77.0 497.5 %all-to-all-start.1 = ((bf16[16,256,2048]{1,2,0:T(8,128)(2,1)}), bf16[16,256,2048]{1,2,0:T(8,128)(2,1)}, u32[]{:S(2)}, u32[]{:S(2)}) async-start(bf16[16,256,2048]{1,2,0:T(8,128)(2,1)} %stack.2), calls=%async_computation.1 | async-start | bytes 33554432 | tf_op jit(solution)/shard_map/all_to_all | solution.py:116
  583.2 4.3 copy-start.2
  660.1 4.3 copy-start.1
